TPU v7x, 64 devices: a 2x2x8 block of a 4x4x8 slice. The times are simulated.
64 devices in a mesh: rep: 8 (over x, y, core), dp: 8 (over z).
Axes of the slice: x: 2, y: 2, z: 8, core: 2. Of those that a mesh axis runs over, the one named last changes fastest.
The devices are a block of a 4x4x8 slice.
Arguments:
- x: bfloat16 [64, 2048, 640], P(('rep', 'dp')), parts along dimension 0
- dy: bfloat16 [64, 2048, 640], P(('rep', 'dp')), parts along dimension 0
- w_gate: bfloat16 [2, 640, 1792], P(None, 'dp')
- w_up: bfloat16 [2, 640, 1792], P(None, 'dp')
- w_down: bfloat16 [2, 1792, 640], P(None, 'dp')
- m_w_gate: float32 [2, 640, 1792], P(None, 'dp')
- m_w_up: float32 [2, 640, 1792], P(None, 'dp')
- m_w_down: float32 [2, 1792, 640], P(None, 'dp')
- v_w_gate: float32 [2, 640, 1792], P(None, 'dp')
- v_w_up: float32 [2, 640, 1792], P(None, 'dp')
- v_w_down: float32 [2, 1792, 640], P(None, 'dp')
Outputs:
- output 1: bfloat16 [16, 640, 1792], P('rep', 'dp'), parts along dimension 0
- output 2: bfloat16 [16, 640, 1792], P('rep', 'dp'), parts along dimension 0
- output 3: bfloat16 [16, 1792, 640], P('rep', 'dp'), parts along dimension 0
- output 4: float32 [16, 640, 1792], P('rep', 'dp'), parts along dimension 0
- output 5: float32 [16, 640, 1792], P('rep', 'dp'), parts along dimension 0
- output 6: float32 [16, 1792, 640], P('rep', 'dp'), parts along dimension 0
- output 7: float32 [16, 640, 1792], P('rep', 'dp'), parts along dimension 0
- output 8: float32 [16, 640, 1792], P('rep', 'dp'), parts along dimension 0
- output 9: float32 [16, 1792, 640], P('rep', 'dp'), parts along dimension 0
There are 8 independent parts. A program takes and returns all parts, laid end to end along the dimension named above; an argument that names none is the same for every part.
All inputs are finite; a program needn't handle non-finite values.
Results may differ from a plain program's by a relative error of at most 0.022.
Values are sent between devices in bfloat16 or wider.
A program may use at most 768 MiB of HBM per device.

v0:
```python
import jax
import jax.numpy as jnp
from jax import lax
from jax.sharding import PartitionSpec as P

NAMES = ("w_gate", "w_up", "w_down")


def matmul(a, w):
    return jnp.dot(a, w, preferred_element_type=jnp.float32).astype(jnp.bfloat16)


def normed(h):
    wide = h.astype(jnp.float32)
    scale = lax.rsqrt(jnp.mean(wide**2, -1, keepdims=True) + 1e-6)
    return (wide * scale).astype(jnp.bfloat16)


def layer(h, w):
    a = normed(h)
    gate = jnp.dot(a, w["w_gate"], preferred_element_type=jnp.float32)
    up = jnp.dot(a, w["w_up"], preferred_element_type=jnp.float32)
    return h + matmul((jax.nn.silu(gate) * up).astype(jnp.bfloat16), w["w_down"])


def adamw(w, m, v, g):
    m = 0.9 * m + 0.1 * g
    v = 0.95 * v + 0.05 * g * g
    step = m * lax.rsqrt(v + 1e-8) + 0.1 * w
    return (w - 0.02 * step).astype(jnp.bfloat16), m, v


def clipped(gradients, sum_of_squares, count):
    factor = jnp.minimum(1.0, 0.5 * lax.rsqrt(sum_of_squares / count + 1e-30))
    return [g * factor for g in gradients]


def solution(mesh):
    def fetched(weights, number):
        return {name: lax.all_gather(w[number], "dp", axis=0, tiled=True) for name, w in zip(NAMES, weights, strict=True)}

    def step(x, dy, *arrays):
        weights, m, v = (arrays[i : i + 3] for i in (0, 3, 6))
        layers = weights[0].shape[0]
        h, kept = x[0], []
        for number in range(layers):
            kept.append(h)
            h = layer(h, fetched(weights, number))
        by_h, mine = dy[0], [None] * layers
        for number in reversed(range(layers)):
            _, back = jax.vjp(lambda w, h: layer(h, w), fetched(weights, number), kept[number])
            by_w, by_h = back(by_h)
            mine[number] = [lax.psum_scatter(by_w[name], "dp", scatter_dimension=0, tiled=True) for name in NAMES]
        gradients = [jnp.stack([mine[number][i] for number in range(layers)]).astype(jnp.float32) for i in range(3)]
        squares = lax.psum(sum(jnp.sum(g * g) for g in gradients), "dp")
        gradients = clipped(gradients, squares, lax.psum(1, "dp") * sum(g.size for g in gradients))
        new = [adamw(w.astype(jnp.float32), m, v, g) for w, m, v, g in zip(weights, m, v, gradients, strict=True)]
        return tuple(one[which] for which in range(3) for one in new)

    states, cut = P(("rep", "dp"), None, None), P(None, "dp", None)
    return jax.shard_map(
        step,
        mesh=mesh,
        in_specs=(states, states) + (cut,) * 9,
        out_specs=(P("rep", "dp", None),) * 9,
        check_vma=False,
    )
```

profile of v0, /device:TPU:22, one launch (start us, length us, event | category | flops | bytes accessed | tf_op | source)
XLA Modules:
  0.0 574.7 jit_solution(4409045992363888428)
XLA Ops:
  22.7 29.6 %all-gather.13.cloned.1.call-done = bf16[1,640,1792]{2,1,0:T(8,128)(2,1)} async-done(((bf16[1,80,1792]{2,1,0:T(8,128)(2,1)}), bf16[1,640,1792]{2,1,0:T(8,128)(2,1)}) %all-gather.13.cloned.1.call-update) | async-done | bytes 2293776 | tf_op jit(solution)/shard_map/all_gather | solution.py:40
  52.3 10.8 %fusion.45 = f32[2048,1792]{1,0:T(8,128)} fusion(bf16[1,640,1792]{2,1,0:T(8,128)(2,1)} %all-gather.13.cloned.1.call-done, bf16[1,2048,640]{1,2,0:T(8,128)(2,1)S(1)} %copy.20, f32[2048]{0:T(1024)S(1)} %add_rsqrt_fusion), kind=kOutput, calls=%fused_computation.65 | convolution fusion | flops 4701552640 | bytes 19603456 | tf_op jit(solution)/shard_map/dot_general | solution.py:21
  63.1 28.0 %all-gather.15.cloned.1.call-done = bf16[1,640,1792]{2,1,0:T(8,128)(2,1)} async-done(((bf16[1,80,1792]{2,1,0:T(8,128)(2,1)}), bf16[1,640,1792]{2,1,0:T(8,128)(2,1)}) %all-gather.15.cloned.1.call-update) | async-done | bytes 2293776 | tf_op jit(solution)/shard_map/all_gather | solution.py:40
  91.1 15.9 %multiply_convert_fusion.1 = (bf16[2048,1792]{1,0:T(8,128)(2,1)}, f32[2048,1792]{1,0:T(8,128)}) fusion(f32[2048,1792]{1,0:T(8,128)} %fusion.45, bf16[1,640,1792]{2,1,0:T(8,128)(2,1)} %all-gather.15.cloned.1.call-done, bf16[1,2048,640]{1,2,0:T(8,128)(2,1)S(1)} %copy.20, f32[2048]{0:T(1024)S(1)} %add_rsqrt_fusion), kind=kOutput, calls=%fused_computation.17 | convolution fusion | flops 4723572736 | bytes 41623552 | tf_op jit(solution)/shard_map/dot_general | solution.py:22
  107.0 22.9 %all-gather.17.cloned.1.call-done = bf16[1,1792,640]{2,1,0:T(8,128)(2,1)} async-done(((bf16[1,224,640]{2,1,0:T(8,128)(2,1)}), bf16[1,1792,640]{2,1,0:T(8,128)(2,1)}) %all-gather.17.cloned.1.call-update) | async-done | bytes 2293776 | tf_op jit(solution)/shard_map/all_gather | solution.py:40
  129.9 10.5 %fusion.19 = (f32[2048]{0:T(1024)S(1)}, bf16[2048,640]{0,1:T(8,128)(2,1)}) fusion(bf16[2048,1792]{1,0:T(8,128)(2,1)} %get-tuple-element.24, bf16[1,1792,640]{2,1,0:T(8,128)(2,1)} %all-gather.17.cloned.1.call-done, bf16[1,2048,640]{1,2,0:T(8,128)(2,1)S(1)} %copy.20), kind=kOutput, calls=%fused_computation.37 | convolution fusion | flops 4704172032 | bytes 14884864 | tf_op jit(solution)/shard_map/dot_general | solution.py:10
  140.4 28.1 %all-gather.21.cloned.1.call-done = bf16[1,1792,640]{2,1,0:T(8,128)(2,1)} async-done(((bf16[1,224,640]{2,1,0:T(8,128)(2,1)}), bf16[1,1792,640]{2,1,0:T(8,128)(2,1)}) %all-gather.21.cloned.1.call-update) | async-done | bytes 2293776 | tf_op jit(solution)/shard_map/all_gather | solution.py:40
  168.5 10.0 %convolution_convert_fusion.1 = bf16[2048,1792]{1,0:T(8,128)(2,1)} fusion(bf16[1,2048,640]{2,1,0:T(8,128)(2,1)} %param.12, bf16[1,1792,640]{2,1,0:T(8,128)(2,1)} %all-gather.21.cloned.1.call-done), kind=kOutput, calls=%fused_computation.27 | convolution fusion | flops 4701290496 | bytes 12255232 | tf_op jit(solution)/shard_map/transpose(jvp())/dot_general | solution.py:10
  178.5 28.6 %all-gather.23.cloned.1.call-done = bf16[1,640,1792]{2,1,0:T(8,128)(2,1)} async-done(((bf16[1,80,1792]{2,1,0:T(8,128)(2,1)}), bf16[1,640,1792]{2,1,0:T(8,128)(2,1)}) %all-gather.23.cloned.1.call-update) | async-done | bytes 2293776 | tf_op jit(solution)/shard_map/all_gather | solution.py:40
  207.1 10.7 %fusion.34 = f32[2048,1792]{1,0:T(8,128)} fusion(bf16[1,640,1792]{2,1,0:T(8,128)(2,1)} %all-gather.23.cloned.1.call-done, bf16[2048,640]{0,1:T(8,128)(2,1)S(1)} %copy-done.3, f32[2048]{0:T(1024)S(1)} %fusion.76), kind=kOutput, calls=%fused_computation.54 | convolution fusion | flops 4701552640 | bytes 19603456 | tf_op jit(solution)/shard_map/jvp()/dot_general | solution.py:22
  217.9 27.9 %all-gather.19.cloned.1.call-done = bf16[1,640,1792]{2,1,0:T(8,128)(2,1)} async-done(((bf16[1,80,1792]{2,1,0:T(8,128)(2,1)}), bf16[1,640,1792]{2,1,0:T(8,128)(2,1)}) %all-gather.19.cloned.1.call-update) | async-done | bytes 2293776 | tf_op jit(solution)/shard_map/all_gather | solution.py:40
  245.8 19.6 %fusion.2 = (bf16[2048,1792]{1,0:T(8,128)(2,1)}, f32[2048,1792]{1,0:T(8,128)}) fusion(f32[2048,1792]{1,0:T(8,128)} %fusion.34, bf16[2048,1792]{1,0:T(8,128)(2,1)} %convolution_convert_fusion.1, bf16[1,640,1792]{2,1,0:T(8,128)(2,1)} %all-gather.19.cloned.1.call-done, bf16[2048,640]{0,1:T(8,128)(2,1)S(1)} %copy-done.3, f32[2048]{0:T(1024)S(1)} %fusion.76), kind=kOutput, calls=%fused_computation.8 | convolution fusion | flops 4745592832 | bytes 48963584 | tf_op jit(solution)/shard_map/jvp()/dot_general | solution.py:21
  265.4 10.8 %fusion.23 = bf16[2048,640]{0,1:T(8,128)(2,1)S(1)} fusion(bf16[2048,1792]{1,0:T(8,128)(2,1)} %convolution_convert_fusion.1, bf16[1,640,1792]{2,1,0:T(8,128)(2,1)} %all-gather.23.cloned.1.call-done, f32[2048,1792]{1,0:T(8,128)} %get-tuple-element.29), kind=kOutput, calls=%fused_computation.41 | convolution fusion | flops 4720951296 | bytes 26935296 | tf_op jit(solution)/shard_map/transpose(jvp())/dot_general | solution.py:22
  285.1 9.6 %convolution_convert_fusion.3 = bf16[1792,640]{1,0:T(8,128)(2,1)} fusion(bf16[2048,1792]{1,0:T(8,128)(2,1)} %get-tuple-element.24, bf16[2048,640]{0,1:T(8,128)(2,1)S(1)} %fusion.29), kind=kOutput, calls=%fused_computation.46 | convolution fusion | flops 4698767360 | bytes 12255232 | tf_op jit(solution)/shard_map/transpose(jvp())/dot_general | solution.py:10
  294.9 13.8 %fusion.22 = bf16[1792,640]{1,0:T(8,128)(2,1)} fusion(f32[2048,1792]{1,0:T(8,128)} %fusion.34, bf16[1,2048,640]{2,1,0:T(8,128)(2,1)S(1)} %copy-done.5, f32[2048,1792]{1,0:T(8,128)} %get-tuple-element.29), kind=kOutput, calls=%fused_computation.40 | convolution fusion | flops 4720787456 | bytes 34275328 | tf_op jit(solution)/shard_map/transpose(jvp())/dot_general | solution.py:10
  320.4 10.6 %fusion.28 = bf16[640,1792]{1,0:T(8,128)(2,1)} fusion(bf16[2048,1792]{1,0:T(8,128)(2,1)S(1)} %convolution_convert_fusion, f32[2048,1792]{1,0:T(8,128)} %fusion.45, bf16[1,2048,640]{1,2,0:T(8,128)(2,1)S(1)} %copy-done.2, f32[2048]{0:T(1024)S(1)} %copy-done.21), kind=kOutput, calls=%fused_computation.44 | convolution fusion | flops 4724719616 | bytes 26943488 | tf_op jit(solution)/shard_map/transpose(jvp())/dot_general | solution.py:22
  331.1 12.3 %fusion.24 = bf16[640,1792]{1,0:T(8,128)(2,1)} fusion(bf16[2048,1792]{1,0:T(8,128)(2,1)} %convolution_convert_fusion.1, bf16[2048,640]{0,1:T(8,128)(2,1)} %get-tuple-element.27, f32[2048]{0:T(1024)S(1)} %fusion.76, f32[2048,1792]{1,0:T(8,128)} %get-tuple-element.29), kind=kOutput, calls=%fused_computation.42 | convolution fusion | flops 4724719616 | bytes 26943488 | tf_op jit(solution)/shard_map/transpose(jvp())/dot_general | solution.py:22
  343.5 17.2 %fusion.25 = bf16[640,1792]{1,0:T(8,128)(2,1)} fusion(f32[2048,1792]{1,0:T(8,128)} %fusion.45, f32[2048,1792]{1,0:T(8,128)} %get-tuple-element.25, bf16[2048,1792]{1,0:T(8,128)(2,1)} %copy-done.23, bf16[1,2048,640]{1,2,0:T(8,128)(2,1)S(1)} %copy-done.2, f32[2048]{0:T(1024)S(1)} %copy-done.21), kind=kOutput, calls=%fused_computation.43 | convolution fusion | flops 4743069696 | bytes 41623552 | tf_op jit(solution)/shard_map/transpose(jvp())/dot_general | solution.py:21
  360.8 10.1 %convolution_convert_fusion.4 = bf16[640,1792]{1,0:T(8,128)(2,1)} fusion(bf16[2048,1792]{1,0:T(8,128)(2,1)} %get-tuple-element.28, bf16[2048,640]{0,1:T(8,128)(2,1)} %get-tuple-element.27, f32[2048]{0:T(1024)S(1)} %fusion.76), kind=kOutput, calls=%fused_computation.47 | convolution fusion | flops 4701552640 | bytes 12263424 | tf_op jit(solution)/shard_map/transpose(jvp())/dot_general | solution.py:21
  376.6 39.3 %reduce-scatter.11.cloned.1.call-done = bf16[80,1792]{1,0:T(8,128)(2,1)} async-done(((bf16[640,1792]{1,0:T(8,128)(2,1)}), bf16[80,1792]{1,0:T(8,128)(2,1)}) %reduce-scatter.11.cloned.1.call-update) | async-done | bytes 286736 | tf_op jit(solution)/shard_map/reduce_scatter | solution.py:53
  415.9 41.1 %reduce-scatter.13.cloned.1.call-done = bf16[80,1792]{1,0:T(8,128)(2,1)} async-done(((bf16[640,1792]{1,0:T(8,128)(2,1)}), bf16[80,1792]{1,0:T(8,128)(2,1)}) %reduce-scatter.13.cloned.1.call-update) | async-done | bytes 286736 | tf_op jit(solution)/shard_map/reduce_scatter | solution.py:53
  458.9 39.3 %reduce-scatter.7.cloned.1.call-done = bf16[80,1792]{1,0:T(8,128)(2,1)} async-done(((bf16[640,1792]{1,0:T(8,128)(2,1)}), bf16[80,1792]{1,0:T(8,128)(2,1)}) %reduce-scatter.7.cloned.1.call-update) | async-done | bytes 286736 | tf_op jit(solution)/shard_map/reduce_scatter | solution.py:53
  498.3 41.1 %reduce-scatter.9.cloned.1.call-done = bf16[80,1792]{1,0:T(8,128)(2,1)} async-done(((bf16[640,1792]{1,0:T(8,128)(2,1)}), bf16[80,1792]{1,0:T(8,128)(2,1)}) %reduce-scatter.9.cloned.1.call-update) | async-done | bytes 286736 | tf_op jit(solution)/shard_map/reduce_scatter | solution.py:53
  543.4 16.2 %psum.7 = f32[]{:T(128)} all-reduce(f32[]{:T(128)S(6)} %add.99), channel_id=1, replica_groups=mesh['rep'=8,'dp'=8] {'dp'}, use_global_device_ids=true, to_apply=%region_12.13 | all-reduce | flops 1 | bytes 8 | tf_op jit(solution)/shard_map/psum | solution.py:55
  (93 shorter events, 53.0 us)
Async XLA Ops:
  7.2 45.1 %all-gather.13.cloned.1.call-start = ((), (), s32[]{:S(2)}) async-start(), calls=%async_computation.12 | async-start | bytes 2580480 | tf_op jit(solution)/shard_map/all_gather | solution.py:40
  9.3 81.8 %all-gather.15.cloned.1.call-start = ((), (), s32[]{:S(2)}) async-start(), calls=%async_computation.13 | async-start | bytes 2580480 | tf_op jit(solution)/shard_map/all_gather | solution.py:40
  11.3 118.6 %all-gather.17.cloned.1.call-start = ((), (), s32[]{:S(2)}) async-start(), calls=%async_computation.14 | async-start | bytes 2580480 | tf_op jit(solution)/shard_map/all_gather | solution.py:40
  12.3 156.2 %all-gather.21.cloned.1.call-start = ((), (), s32[]{:S(2)}) async-start(), calls=%async_computation.16 | async-start | bytes 2580480 | tf_op jit(solution)/shard_map/all_gather | solution.py:40
  12.9 194.2 %all-gather.23.cloned.1.call-start = ((), (), s32[]{:S(2)}) async-start(), calls=%async_computation.17 | async-start | bytes 2580480 | tf_op jit(solution)/shard_map/all_gather | solution.py:40
  13.6 232.2 %all-gather.19.cloned.1.call-start = ((), (), s32[]{:S(2)}) async-start(), calls=%async_computation.15 | async-start | bytes 2580480 | tf_op jit(solution)/shard_map/all_gather | solution.py:40
  14.2 356.9 %reduce-scatter.15.cloned.1.call-start = ((), (), s32[]{:S(2)}) async-start(), calls=%async_computation.10 | async-start | bytes 2580480 | tf_op jit(solution)/shard_map/reduce_scatter | solution.py:53
  17.3 112.6 %copy-start.1 = (bf16[1,2048,640]{1,2,0:T(8,128)(2,1)}, bf16[1,2048,640]{1,2,0:T(8,128)(2,1)S(1)}, u32[]{:S(2)}) copy-start(bf16[1,2048,640]{1,2,0:T(8,128)(2,1)S(1)} %copy.20) | copy-start | bytes 7864324
  17.9 73.2 %copy-start.20 = (f32[2048]{0:T(1024)}, f32[2048]{0:T(1024)S(1)}, u32[]{:S(2)}) copy-start(f32[2048]{0:T(1024)S(1)} %add_rsqrt_fusion) | copy-start | bytes 24580
  140.4 66.7 %copy-start.3 = (bf16[2048,640]{0,1:T(8,128)(2,1)S(1)}, bf16[2048,640]{0,1:T(8,128)(2,1)}, u32[]{:S(2)}) copy-start(bf16[2048,640]{0,1:T(8,128)(2,1)} %get-tuple-element.27) | copy-start | bytes 7864324
  265.4 10.8 %copy-start.22 = (bf16[1,640,1792]{2,1,0:T(8,128)(2,1)S(1)}, bf16[1,640,1792]{2,1,0:T(8,128)(2,1)}, u32[]{:S(2)}) copy-start(bf16[1,640,1792]{2,1,0:T(8,128)(2,1)} %all-gather.19.cloned.1.call-done) | copy-start | bytes 6881284
  265.4 10.8 %copy-start.24 = (bf16[2048,1792]{1,0:T(8,128)(2,1)S(1)}, bf16[2048,1792]{1,0:T(8,128)(2,1)}, u32[]{:S(2)}) copy-start(bf16[2048,1792]{1,0:T(8,128)(2,1)} %get-tuple-element.28) | copy-start | bytes 22020100
  294.8 79.8 %reduce-scatter.17.cloned.1.call-start = ((), (), s32[]{:S(2)}) async-start(), calls=%async_computation.11 | async-start | bytes 2580480 | tf_op jit(solution)/shard_map/reduce_scatter | solution.py:53
  308.8 11.7 %copy-start.2 = (bf16[1,2048,640]{1,2,0:T(8,128)(2,1)S(1)}, bf16[1,2048,640]{1,2,0:T(8,128)(2,1)}, u32[]{:S(2)}) copy-start(bf16[1,2048,640]{1,2,0:T(8,128)(2,1)} %copy-done.1) | copy-start | bytes 7864324
  308.8 11.7 %copy-start.21 = (f32[2048]{0:T(1024)S(1)}, f32[2048]{0:T(1024)}, u32[]{:S(2)}) copy-start(f32[2048]{0:T(1024)} %copy-done.20) | copy-start | bytes 24580
  308.8 107.1 %reduce-scatter.11.cloned.1.call-start = ((), (), s32[]{:S(2)}) async-start(), calls=%async_computation.8 | async-start | bytes 2580480 | tf_op jit(solution)/shard_map/reduce_scatter | solution.py:53
  331.1 125.9 %reduce-scatter.13.cloned.1.call-start = ((), (), s32[]{:S(2)}) async-start(), calls=%async_computation.9 | async-start | bytes 2580480 | tf_op jit(solution)/shard_map/reduce_scatter | solution.py:53
  343.5 154.8 %reduce-scatter.7.cloned.1.call-start = ((), (), s32[]{:S(2)}) async-start(), calls=%async_computation.6 | async-start | bytes 2580480 | tf_op jit(solution)/shard_map/reduce_scatter | solution.py:53
  360.8 178.6 %reduce-scatter.9.cloned.1.call-start = ((), (), s32[]{:S(2)}) async-start(), calls=%async_computation.7 | async-start | bytes 2580480 | tf_op jit(solution)/shard_map/reduce_scatter | solution.py:53
  371.0 189.2 %copy-start.7 = (bf16[2,224,640]{2,1,0:T(8,128)(2,1)S(1)}, bf16[2,224,640]{2,1,0:T(8,128)(2,1)}, u32[]{:S(2)}) copy-start(bf16[2,224,640]{2,1,0:T(8,128)(2,1)} %param.15) | copy-start | bytes 1720324
  371.0 189.3 %copy-start.10 = (f32[2,224,640]{2,1,0:T(8,128)S(1)}, f32[2,224,640]{2,1,0:T(8,128)}, u32[]{:S(2)}) copy-start(f32[2,224,640]{2,1,0:T(8,128)} %param.21) | copy-start | bytes 3440644
  371.0 189.3 %copy-start.11 = (f32[2,224,640]{2,1,0:T(8,128)S(1)}, f32[2,224,640]{2,1,0:T(8,128)}, u32[]{:S(2)}) copy-start(f32[2,224,640]{2,1,0:T(8,128)} %param.18) | copy-start | bytes 3440644
  539.4 24.0 %copy-start.18 = (bf16[80,1792]{1,0:T(8,128)(2,1)S(1)}, bf16[80,1792]{1,0:T(8,128)(2,1)}, u32[]{:S(2)}) copy-start(bf16[80,1792]{1,0:T(8,128)(2,1)} %reduce-scatter.7.cloned.1.call-done) | copy-start | bytes 860164
  539.4 24.0 %copy-start.19 = (bf16[80,1792]{1,0:T(8,128)(2,1)S(1)}, bf16[80,1792]{1,0:T(8,128)(2,1)}, u32[]{:S(2)}) copy-start(bf16[80,1792]{1,0:T(8,128)(2,1)} %reduce-scatter.9.cloned.1.call-done) | copy-start | bytes 860164
  (13 other events, 51.2 us)
Sparse Core Ops, SparseCore 0:
  10.2 42.0 all-gather.12
  54.4 36.5 all-gather.14
  93.2 36.5 all-gather.16
  131.9 36.5 all-gather.20
  170.5 36.5 all-gather.22
  209.1 36.5 all-gather.18
  294.9 38.4 reduce-scatter.14
  335.7 38.8 reduce-scatter.16
  377.0 38.8 reduce-scatter.10
  418.1 38.8 reduce-scatter.12
  459.4 38.8 reduce-scatter.6
  500.5 38.8 reduce-scatter.8
where the time goes:
time: 582 us; the launch traced here: 575 us
  waiting for transfers between devices  332 us (57%)
  matrix products  176 us (30%)
  local copies, waits for them, and re-layouts  17.9 us (3%)
  between operations  17.6 us (3%)
  blocking collectives  16.2 us (3%)
  other arithmetic  14.5 us (2%)
    all_gather x6, waiting for transfers between devices, fetched(): lax.all_gather(w[number], 'dp', axis=0, tiled=True)  165 us
    reduce_scatter x6, waiting for transfers between devices, step(): lax.psum_scatter(by_w[name], 'dp', scatter_dimension=0, tiled=True)  164 us
    dot_general x5, matrix products, layer(): gate = jnp.dot(a, w['w_gate'], preferred_element_type=jnp.float32)  63.2 us
    dot_general x5, matrix products, layer(): up = jnp.dot(a, w['w_up'], preferred_element_type=jnp.float32)  60.3 us
    dot_general x5, matrix products, matmul(): jnp.dot(a, w, preferred_element_type=jnp.float32).astype(jnp.bfloat16)  52.5 us
    psum x1, blocking collectives, step(): squares = lax.psum(sum((jnp.sum(g * g) for g in gradients)), 'dp')  16.2 us
    unnamed x52, local copies, waits for them, and re-layouts  13.3 us
  transfers between devices with their start and end apart: 12, of which 11 were waited for; matrix products, arithmetic and copies ran while one was open for 25% of the time, Pallas kernels for 0%

commit v1 on v0

v1 whole, which is shorter than its diff:
```python
import functools

import jax
import jax.numpy as jnp
from jax import lax
from jax.experimental import pallas as pl
from jax.experimental.pallas import tpu as pltpu
from jax.sharding import PartitionSpec as P

F32, BF16 = jnp.float32, jnp.bfloat16
MESH = pl.DeviceIdType.MESH
CHUNK = 256
TILE = 512
SMALL = 256


def dot(a, b):
    return jnp.dot(a, b, preferred_element_type=F32)


def dot_t(a, b):
    return lax.dot_general(a, b, (((1,), (1,)), ((), ())), preferred_element_type=F32)


def scale_of(wide):
    return lax.rsqrt(jnp.mean(wide * wide, -1, keepdims=True) + 1e-6)


def kernel(n, dims, x_hbm, dy_hbm, wg_hbm, wu_hbm, wd_hbm, gg_hbm, gu_hbm, gd_hbm, total_ref,
           wgu, wd, dgu, dd, h, dy, a, at, dyt, acc, hid, dgdu, gu_slot, dn_slot, squares, mine,
           load_sem, out_sem, zrecv, zsend, drecv, dsend, gu_recv, gu_send, dn_recv, dn_send, sq_recv, sq_send):
    tokens, d, ff, rows, down = dims
    half = down // 2
    chunks = ff // CHUNK
    me = lax.axis_index("dp")
    rep = lax.axis_index("rep")
    core = lax.rem(rep, 2)
    partner = rep + 1 - 2 * core
    ahead = (lax.rem(me + 1, n), lax.rem(me + n - 1, n))

    def to(direction):
        return {"dp": ahead[direction]}

    loads = []
    for layer in range(2):
        for which, src in enumerate((wg_hbm, wu_hbm)):
            dst = wgu.at[layer, which, pl.ds(pl.multiple_of(me * rows, 16), rows), :]
            loads.append(pltpu.make_async_copy(src.at[layer], dst, load_sem.at[len(loads)]))
        dst = wd.at[layer, pl.ds(pl.multiple_of(me * down, 16), down), :]
        loads.append(pltpu.make_async_copy(wd_hbm.at[layer], dst, load_sem.at[len(loads)]))
    loads.append(pltpu.make_async_copy(x_hbm.at[0], h, load_sem.at[6]))
    loads.append(pltpu.make_async_copy(dy_hbm.at[0], dy, load_sem.at[7]))
    for one in loads:
        one.start()
    barrier = pltpu.get_barrier_semaphore()
    for k in range(1, n):
        pl.semaphore_signal(barrier, inc=1, device_id={"dp": lax.rem(me + k, n)}, device_id_type=MESH)
    pl.semaphore_signal(barrier, inc=1, device_id={"rep": partner}, device_id_type=MESH)
    pl.semaphore_wait(barrier, n)
    for one in loads:
        one.wait()

    def piece(layer, which, number, direction, block):
        if number < 2:
            wide = ff // 2
            cut = (wide // 128 + 1) // 2 * 128
            off, size = (0, cut) if number == 0 else (cut, wide - cut)
            return wgu.at[layer, which, pl.ds(pl.multiple_of(block * rows, 16), rows), pl.ds(direction * wide + off, size)]
        cut = (half // 16 + 1 - layer) // 2 * 16
        off, size = (0, cut) if direction == 0 else (cut, half - cut)
        return wd.at[layer, pl.ds(pl.multiple_of(block * down + which * half + off, 16), size), :]

    def held(direction, t):
        return lax.rem(me - t + n, n) if direction == 0 else lax.rem(me + t, n)

    def along(layer, number, direction, t):
        ref = piece(layer, core, number, direction, held(direction, t))
        slot = lax.rem(t, 2)
        return pltpu.make_async_remote_copy(ref, ref, zsend.at[layer, number, direction, slot], zrecv.at[layer, number, direction, slot],
                                            device_id=to(direction), device_id_type=MESH)

    def across(layer, which, number, direction, t):
        ref = piece(layer, which, number, direction, held(direction, t))
        slot = lax.rem(t, 2)
        return pltpu.make_async_remote_copy(ref, ref, dsend.at[layer, number, direction, slot], drecv.at[layer, number, direction, slot],
                                            device_id={"rep": partner}, device_id_type=MESH)

    def arrived(layer, number, direction, t):
        ref = piece(layer, core, number, direction, held(direction, t))
        slot = lax.rem(t + 1, 2)
        return pltpu.make_async_remote_copy(ref, ref, zsend.at[layer, number, direction, slot], zrecv.at[layer, number, direction, slot],
                                            device_id=to(direction), device_id_type=MESH)

    def gather_round(layer, t):
        for number in range(3):
            for direction in range(2):
                @pl.when(t >= 1)
                def _():
                    arrived(layer, number, direction, t).wait_recv()

                @pl.when((t >= 2) & (t < n))
                def _():
                    across(layer, 1 - core, number, direction, t - 1).wait_recv()

            for direction in range(2):
                @pl.when((t >= 2) & (t <= n - 2))
                def _():
                    along(layer, number, direction, t - 2).wait_send()

                @pl.when(t <= n - 2)
                def _():
                    along(layer, number, direction, t).start()

                @pl.when(t >= 3)
                def _():
                    across(layer, core, number, direction, t - 2).wait_send()

                @pl.when(t >= 1)
                def _():
                    across(layer, core, number, direction, t).start()

    def gather_end(layer):
        for number in range(3):
            for direction in range(2):
                across(layer, 1 - core, number, direction, n - 1).wait_recv()
                for t in (n - 3, n - 2):
                    along(layer, number, direction, t).wait_send()
                for t in (n - 2, n - 1):
                    across(layer, core, number, direction, t).wait_send()

    def small(k):
        return pl.ds(pl.multiple_of(k * SMALL, SMALL), SMALL)

    steps = tokens // SMALL

    def first(t, _):
        gather_round(0, t)

        @pl.when(t < steps)
        def _():
            wide = h[small(t), :].astype(F32)
            a[0, small(t), :] = (wide * scale_of(wide)).astype(BF16)
            dyt[:, small(t)] = dy[small(t), :].T
        return 0

    lax.fori_loop(0, max(n, steps), first, 0)
    gather_end(0)

    def cols(c):
        return pl.ds(pl.multiple_of(c * CHUNK, CHUNK), CHUNK)

    def forward(c, _):
        gather_round(1, c)

        def tile(k, _):
            r = pl.ds(pl.multiple_of(k * TILE, TILE), TILE)
            gate = dot(a[0, r, :], wgu[0, 0, :, cols(c)])
            up = dot(a[0, r, :], wgu[0, 1, :, cols(c)])
            hidden = (gate * jax.nn.sigmoid(gate) * up).astype(BF16)
            out = dot(hidden, wd[0, cols(c), :])

            @pl.when(c == 0)
            def _():
                acc[r, :] = out

            @pl.when(c > 0)
            def _():
                acc[r, :] += out
            return 0

        lax.fori_loop(0, tokens // TILE, tile, 0)
        return 0

    lax.fori_loop(0, chunks, forward, 0)
    for t in range(chunks, n):
        gather_round(1, t)

    def between(k, _):
        r = small(k)
        h1 = (h[r, :].astype(F32) + acc[r, :].astype(BF16).astype(F32)).astype(BF16)
        h[r, :] = h1
        wide = h1.astype(F32)
        a1 = (wide * scale_of(wide)).astype(BF16)
        a[1, r, :] = a1
        at[:, r] = a1.T
        return 0

    lax.fori_loop(0, steps, between, 0)
    gather_end(1)

    slabs = 2 * chunks

    def block_at(direction, t):
        return lax.rem(me - 1 - t + 2 * n, n) if direction == 0 else lax.rem(me + 1 + t, n)

    def gu_ref(j, direction, t):
        layer = 1 - j // chunks
        r = pl.ds(pl.multiple_of(block_at(direction, t) * rows, 16), rows)
        return dgu.at[layer, direction, r, cols(lax.rem(j, chunks))]

    def gu_copy(r, direction, t):
        slot = lax.rem(r, 2)
        return pltpu.make_async_remote_copy(gu_ref(r - t, direction, t), gu_slot.at[direction, slot, t], gu_send.at[direction, t],
                                            gu_recv.at[direction, slot, t], device_id=to(direction), device_id_type=MESH)

    def gu_round(r):
        def tick(k, _):
            t = n - 1 - k
            j = r - t

            @pl.when((j >= 0) & (j < slabs))
            def _():
                @pl.when(t >= 1)
                def _():
                    for direction in range(2):
                        gu_copy(r - 1, direction, t - 1).wait_recv()
                        mine_ref = gu_ref(j, direction, t)
                        got = gu_slot[direction, lax.rem(r + 1, 2), t - 1].astype(F32)
                        mine_ref[...] = (got + mine_ref[...].astype(F32)).astype(BF16)

            @pl.when((t <= n - 2) & (j >= 1) & (j <= slabs))
            def _():
                for direction in range(2):
                    gu_copy(r - 1, direction, t).wait_send()

            @pl.when((j >= 0) & (j < slabs) & (t <= n - 2))
            def _():
                for direction in range(2):
                    gu_copy(r, direction, t).start()
            return 0

        lax.fori_loop(0, n, tick, 0)

    parts = d // 128

    def dn_ref(layer, s, direction, t):
        r = pl.ds(pl.multiple_of(block_at(direction, t) * down + direction * half, 16), half)
        return dd.at[layer, r, pl.ds(pl.multiple_of(s * 128, 128), 128)]

    def dn_copy(layer, s, direction, t):
        slot = lax.rem(t, 2)
        return pltpu.make_async_remote_copy(dn_ref(layer, s, direction, t), dn_slot.at[layer, direction, slot, s], dn_send.at[layer, direction, s],
                                            dn_recv.at[layer, direction, slot, s], device_id=to(direction), device_id_type=MESH)

    def dn_round(layer, t):
        def part(s, _):
            @pl.when(t >= 1)
            def _():
                for direction in range(2):
                    dn_copy(layer, s, direction, t - 1).wait_recv()
                    mine_ref = dn_ref(layer, s, direction, t)
                    got = dn_slot[layer, direction, lax.rem(t + 1, 2), s].astype(F32)
                    mine_ref[...] = (got + mine_ref[...].astype(F32)).astype(BF16)
                for direction in range(2):
                    dn_copy(layer, s, direction, t - 1).wait_send()

            @pl.when(t <= n - 2)
            def _():
                for direction in range(2):
                    dn_copy(layer, s, direction, t).start()
            return 0

        lax.fori_loop(0, parts, part, 0)

    def backward(layer, c):
        def tile(k, _):
            r = pl.ds(pl.multiple_of(k * TILE, TILE), TILE)
            gate = dot(a[layer, r, :], wgu[layer, 0, :, cols(c)])
            up = dot(a[layer, r, :], wgu[layer, 1, :, cols(c)])
            by = dot_t(dy[r, :], wd[layer, cols(c), :]).astype(BF16).astype(F32)
            sig = jax.nn.sigmoid(gate)
            silu = gate * sig
            hid[r, :] = (silu * up).astype(BF16)
            by_gate = (by * up * (sig + silu * (1.0 - sig))).astype(BF16)
            by_up = (by * silu).astype(BF16)
            dgdu[r, pl.ds(0, CHUNK)] = by_gate
            dgdu[r, pl.ds(CHUNK, CHUNK)] = by_up
            if layer == 1:
                out = dot_t(by_gate, wgu[layer, 0, :, cols(c)]) + dot_t(by_up, wgu[layer, 1, :, cols(c)])

                @pl.when(c == 0)
                def _():
                    acc[r, :] = out

                @pl.when(c > 0)
                def _():
                    acc[r, :] += out
            return 0

        lax.fori_loop(0, tokens // TILE, tile, 0)
        by_w = dot(at[...], dgdu[...])
        dgu[layer, 0, :, cols(c)] = by_w[:, :CHUNK].astype(BF16)
        dgu[layer, 1, :, cols(c)] = by_w[:, CHUNK:].astype(BF16)
        dd[layer, cols(c), :] = dot(dyt[...], hid[...]).T.astype(BF16)

    def last_layer(c, _):
        backward(1, c)
        gu_round(c)
        return 0

    lax.fori_loop(0, chunks, last_layer, 0)

    def norm_back(k, _):
        r = small(k)
        by_a = acc[r, :].astype(BF16).astype(F32)
        wide = h[r, :].astype(F32)
        scale = scale_of(wide)
        by_scale = jnp.sum(by_a * wide, -1, keepdims=True)
        by_wide = by_a * scale - wide * (scale * scale * scale * by_scale * (1.0 / d))
        by_h = (dy[r, :].astype(F32) + by_wide.astype(BF16).astype(F32)).astype(BF16)
        dy[r, :] = by_h
        dyt[:, r] = by_h.T
        at[:, r] = a[0, r, :].T
        return 0

    lax.fori_loop(0, steps, norm_back, 0)

    def first_layer(c, _):
        backward(0, c)
        gu_round(chunks + c)
        dn_round(1, c)
        return 0

    lax.fori_loop(0, chunks, first_layer, 0)
    for t in range(chunks, n):
        dn_round(1, t)

    def drain(k, _):
        gu_round(2 * chunks + k)
        dn_round(0, k)
        return 0

    lax.fori_loop(0, n, drain, 0)

    outs = []
    for layer in range(2):
        for which, dst in enumerate((gg_hbm, gu_hbm)):
            src = dgu.at[layer, which, pl.ds(pl.multiple_of(me * rows, 16), rows), :]
            outs.append(pltpu.make_async_copy(src, dst.at[layer], out_sem.at[len(outs)]))
        src = dd.at[layer, pl.ds(pl.multiple_of(me * down, 16), down), :]
        outs.append(pltpu.make_async_copy(src, gd_hbm.at[layer], out_sem.at[len(outs)]))
    for one in outs:
        one.start()
    sums = jnp.zeros((1, 1), F32)
    for layer in range(2):
        for which in range(2):
            v = dgu[layer, which, pl.ds(pl.multiple_of(me * rows, 16), rows), :].astype(F32)
            sums += jnp.sum(v * v, keepdims=True)
        v = dd[layer, pl.ds(pl.multiple_of(me * down, 16), down), :].astype(F32)
        sums += jnp.sum(v * v, keepdims=True)
    mine[...] = jnp.broadcast_to(sums, mine.shape)

    def spread(k):
        return pltpu.make_async_remote_copy(mine, squares.at[k - 1], sq_send.at[k - 1], sq_recv.at[k - 1],
                                            device_id={"dp": lax.rem(me + k, n)}, device_id_type=MESH)

    for k in range(1, n):
        spread(k).start()
    for k in range(1, n):
        spread(k).wait_recv()
    total = mine[...]
    for k in range(1, n):
        total += squares[k - 1]
    total_ref[...] = total
    for k in range(1, n):
        spread(k).wait_send()
    for one in outs:
        one.wait()


def summed_gradients(n, x, dy, w_gate, w_up, w_down):
    _, tokens, d = x.shape
    layers, rows, ff = w_gate.shape
    down = w_down.shape[1]
    dims = (tokens, d, ff, rows, down)
    half = down // 2
    dma = pltpu.SemaphoreType.DMA
    anywhere = pl.BlockSpec(memory_space=pl.ANY)
    return pl.pallas_call(
        functools.partial(kernel, n, dims),
        out_shape=(
            jax.ShapeDtypeStruct(w_gate.shape, BF16),
            jax.ShapeDtypeStruct(w_up.shape, BF16),
            jax.ShapeDtypeStruct(w_down.shape, BF16),
            jax.ShapeDtypeStruct((8, 128), F32),
        ),
        in_specs=[anywhere] * 5,
        out_specs=(anywhere,) * 3 + (pl.BlockSpec(memory_space=pltpu.VMEM),),
        scratch_shapes=[
            pltpu.VMEM((layers, 2, d, ff), BF16),
            pltpu.VMEM((layers, ff, d), BF16),
            pltpu.VMEM((layers, 2, d, ff), BF16),
            pltpu.VMEM((layers, ff, d), BF16),
            pltpu.VMEM((tokens, d), BF16),
            pltpu.VMEM((tokens, d), BF16),
            pltpu.VMEM((layers, tokens, d), BF16),
            pltpu.VMEM((d, tokens), BF16),
            pltpu.VMEM((d, tokens), BF16),
            pltpu.VMEM((tokens, d), F32),
            pltpu.VMEM((tokens, CHUNK), BF16),
            pltpu.VMEM((tokens, 2 * CHUNK), BF16),
            pltpu.VMEM((2, 2, n - 1, rows, CHUNK), BF16),
            pltpu.VMEM((2, 2, 2, d // 128, half, 128), BF16),
            pltpu.VMEM((n - 1, 8, 128), F32),
            pltpu.VMEM((8, 128), F32),
            dma((8,)),
            dma((6,)),
            dma((2, 3, 2, 2)),
            dma((2, 3, 2, 2)),
            dma((2, 3, 2, 2)),
            dma((2, 3, 2, 2)),
            dma((2, 2, n - 1)),
            dma((2, n - 1)),
            dma((2, 2, 2, d // 128)),
            dma((2, 2, d // 128)),
            dma((n - 1,)),
            dma((n - 1,)),
        ],
        compiler_params=pltpu.CompilerParams(collective_id=0, has_side_effects=True, vmem_limit_bytes=67_000_000),
    )(x, dy, w_gate, w_up, w_down)


def adamw(w, m, v, g):
    m = 0.9 * m + 0.1 * g
    v = 0.95 * v + 0.05 * g * g
    step = m * lax.rsqrt(v + 1e-8) + 0.1 * w
    return (w - 0.02 * step).astype(BF16), m, v


def solution(mesh):
    n = mesh.shape["dp"]

    def step(x, dy, *arrays):
        weights, m, v = (arrays[i : i + 3] for i in (0, 3, 6))
        *gradients, squares = summed_gradients(n, x, dy, *weights)
        count = n * sum(g.size for g in gradients)
        factor = jnp.minimum(1.0, 0.5 * lax.rsqrt(squares[0, 0] / count + 1e-30))
        new = [adamw(w.astype(F32), m, v, g.astype(F32) * factor) for w, m, v, g in zip(weights, m, v, gradients, strict=True)]
        return tuple(one[which] for which in range(3) for one in new)

    states, cut = P(("rep", "dp"), None, None), P(None, "dp", None)
    return jax.shard_map(
        step,
        mesh=mesh,
        in_specs=(states, states) + (cut,) * 9,
        out_specs=(P("rep", "dp", None),) * 9,
        check_vma=False,
    )
```

time: 582 us -> 304 us (0.52); the launches traced: 575 us -> 303 us
  waiting for transfers between devices: 332 us -> 0 us
  Pallas kernels: 0 us -> 293 us
  matrix products: 176 us -> 0 us
  local copies, waits for them, and re-layouts: 17.9 us -> 1.22 us
  between operations: 17.6 us -> 1.4 us
  blocking collectives: 16.2 us -> 0 us
  other arithmetic: 14.5 us -> 8.11 us
    pallas_call x0 -> x1, Pallas kernels: none -> 293 us  [summed_gradients(): pl.pallas_call(functools.partial(kernel, n, dims), out_shape=(jax.ShapeDt...]
    dot_general x15 -> x0, matrix products: 176 us -> none  [the longest x5 63.2 us: layer(): gate = jnp.dot(a, w['w_gate'], preferred_element_type=jnp.float32)]
    all_gather x6 -> x0, waiting for transfers between devices: 165 us -> none  [fetched(): lax.all_gather(w[number], 'dp', axis=0, tiled=True)]
    reduce_scatter x6 -> x0, waiting for transfers between devices: 164 us -> none  [step(): lax.psum_scatter(by_w[name], 'dp', scatter_dimension=0, tiled=True)]
    psum x1 -> x0, blocking collectives: 16.2 us -> none  [step(): squares = lax.psum(sum((jnp.sum(g * g) for g in gradients)), 'dp')]
    unnamed x52 -> x8, local copies, waits for them, and re-layouts: 13.3 us -> 0.02 us
    reduce_sum x4 -> x0, other arithmetic: 6.45 us -> none  [the longest x3 5.89 us: step(): squares = lax.psum(sum((jnp.sum(g * g) for g in gradients)), 'dp')]
  transfers between devices with their start and end apart: 12 -> 0, of which waited for: 11 -> 0; matrix products, arithmetic and copies ran while one was open for 25% -> 0% of each run, Pallas kernels for 0% -> 0%
where the time goes in v1:
time: 304 us; the launch traced here: 303 us
  Pallas kernels  293 us (96%)
  other arithmetic  8.11 us (3%)
    pallas_call x1, Pallas kernels, summed_gradients(): pl.pallas_call(functools.partial(kernel, n, dims), out_shape=(jax.ShapeDt...  293 us
    convert_element_type x2, other arithmetic, adamw(): return ((w - 0.02 * step).astype(BF16), m, v)  8.11 us

profile of v1, /device:TPU:22, one launch (start us, length us, event | category | flops | bytes accessed | tf_op | source)
XLA Modules:
  0.0 303.4 jit_solution(9510071725364911994)
XLA Ops:
  0.6 292.7 %shard_map.178 = (bf16[2,80,1792]{2,1,0:T(8,128)(2,1)}, bf16[2,80,1792]{2,1,0:T(8,128)(2,1)}, bf16[2,224,640]{2,1,0:T(8,128)(2,1)}, f32[8,128]{1,0:T(8,128)}) custom-call(bf16[1,2048,640]{2,1,0:T(8,128)(2,1)} %x_hbm.1, bf16[1,2048,640]{2,1,0:T(8,128)(2,1)} %dy_hbm.1, bf16[2,80,1792]{2,1,0:T(8,128)(2,1)} %wg_hbm.1, bf16[2,80,1792]{2,1,0:T(8,128)(2,1)} %wu_hbm.1, ...), custom_call_target="tpu_custom_call" | custom-call | tf_op jit(solution)/shard_map/pallas_call | solution.py:379
  293.3 1.2 slice.3
  295.2 0.0 copy-start
  295.2 0.0 copy-start.1
  295.2 0.0 copy-start.2
  295.2 0.0 copy-start.3
  295.3 6.2 %fusion.2 = (bf16[2,80,1792]{2,1,0:T(8,128)(2,1)}, f32[2,80,1792]{2,1,0:T(8,128)}, f32[2,80,1792]{2,1,0:T(8,128)}, bf16[2,80,1792]{2,1,0:T(8,128)(2,1)}, f32[2,80,1792]{2,1,0:T(8,128)}, /*index=5*/f32[2,80,1792]{2,1,0:T(8,128)}) fusion(bf16[2,80,1792]{2,1,0:T(8,128)(2,1)} %wg_hbm.1, f32[]{:T(128)} %bitcast, bf16[2,80,1792]{2,1,0:T(8,128)(2,1)} %get-tuple-element.13, ...), kind=kLoop, calls=%fused_computation.11 | loop fusion | flops 9748480 | bytes 12615684 | tf_op jit(solution)/shard_map/convert_element_type | solution.py:427
  301.5 0.0 copy-done
  301.5 0.0 copy-done.1
  301.5 0.0 copy-done.2
  301.5 0.0 copy-done.3
  301.5 1.9 fusion.8
Async XLA Ops:
  295.2 6.3 %copy-start = (bf16[2,224,640]{2,1,0:T(8,128)(2,1)S(1)}, bf16[2,224,640]{2,1,0:T(8,128)(2,1)}, u32[]{:S(2)}) copy-start(bf16[2,224,640]{2,1,0:T(8,128)(2,1)} %wd_hbm.1) | copy-start | bytes 1720324
  295.2 6.2 %copy-start.1 = (f32[2,224,640]{2,1,0:T(8,128)S(1)}, f32[2,224,640]{2,1,0:T(8,128)}, u32[]{:S(2)}) copy-start(f32[2,224,640]{2,1,0:T(8,128)} %param.21) | copy-start | bytes 3440644
  295.2 6.2 %copy-start.2 = (f32[2,224,640]{2,1,0:T(8,128)S(1)}, f32[2,224,640]{2,1,0:T(8,128)}, u32[]{:S(2)}) copy-start(f32[2,224,640]{2,1,0:T(8,128)} %param.18) | copy-start | bytes 3440644
  295.2 6.2 %copy-start.3 = (bf16[2,224,640]{2,1,0:T(8,128)(2,1)S(1)}, bf16[2,224,640]{2,1,0:T(8,128)(2,1)}, u32[]{:S(2)}) copy-start(bf16[2,224,640]{2,1,0:T(8,128)(2,1)} %get-tuple-element.16) | copy-start | bytes 1720324

commit v2 on v1

--- a/solution.py
+++ b/solution.py
@@ -57,7 +57,7 @@
         pl.semaphore_signal(barrier, inc=1, device_id={"dp": lax.rem(me + k, n)}, device_id_type=MESH)
     pl.semaphore_signal(barrier, inc=1, device_id={"rep": partner}, device_id_type=MESH)
     pl.semaphore_wait(barrier, n)
-    for one in loads:
+    for one in loads[:6]:
         one.wait()
 
     def piece(layer, which, number, direction, block):
@@ -133,14 +133,21 @@
 
     steps = tokens // SMALL
 
+    gather_round(0, 0)
+    for one in loads[6:]:
+        one.wait()
+
     def first(t, _):
-        gather_round(0, t)
+        @pl.when(t >= 1)
+        def _():
+            gather_round(0, t)
 
         @pl.when(t < steps)
         def _():
             wide = h[small(t), :].astype(F32)
             a[0, small(t), :] = (wide * scale_of(wide)).astype(BF16)
             dyt[:, small(t)] = dy[small(t), :].T
+            acc[small(t), :] = jnp.zeros((SMALL, d), F32)
         return 0
 
     lax.fori_loop(0, max(n, steps), first, 0)
@@ -154,18 +161,10 @@
 
         def tile(k, _):
             r = pl.ds(pl.multiple_of(k * TILE, TILE), TILE)
-            gate = dot(a[0, r, :], wgu[0, 0, :, cols(c)])
-            up = dot(a[0, r, :], wgu[0, 1, :, cols(c)])
+            both = dot(a[0, r, :], jnp.concatenate([wgu[0, 0, :, cols(c)], wgu[0, 1, :, cols(c)]], 1))
+            gate, up = both[:, :CHUNK], both[:, CHUNK:]
             hidden = (gate * jax.nn.sigmoid(gate) * up).astype(BF16)
-            out = dot(hidden, wd[0, cols(c), :])
-
-            @pl.when(c == 0)
-            def _():
-                acc[r, :] = out
-
-            @pl.when(c > 0)
-            def _():
-                acc[r, :] += out
+            acc[r, :] += dot(hidden, wd[0, cols(c), :])
             return 0
 
         lax.fori_loop(0, tokens // TILE, tile, 0)
@@ -183,6 +182,7 @@
         a1 = (wide * scale_of(wide)).astype(BF16)
         a[1, r, :] = a1
         at[:, r] = a1.T
+        acc[r, :] = jnp.zeros((SMALL, d), F32)
         return 0
 
     lax.fori_loop(0, steps, between, 0)
@@ -198,38 +198,36 @@
         r = pl.ds(pl.multiple_of(block_at(direction, t) * rows, 16), rows)
         return dgu.at[layer, direction, r, cols(lax.rem(j, chunks))]
 
-    def gu_copy(r, direction, t):
-        slot = lax.rem(r, 2)
-        return pltpu.make_async_remote_copy(gu_ref(r - t, direction, t), gu_slot.at[direction, slot, t], gu_send.at[direction, t],
+    def gu_copy(j, direction, t):
+        slot = lax.rem(j, 2)
+        return pltpu.make_async_remote_copy(gu_ref(j, direction, t), gu_slot.at[direction, slot, t], gu_send.at[direction, slot, t],
                                             gu_recv.at[direction, slot, t], device_id=to(direction), device_id_type=MESH)
 
     def gu_round(r):
         def tick(k, _):
-            t = n - 1 - k
-            j = r - t
+            i = n // 2 - 1 - k
+            t = lax.rem(r, 2) + 2 * i
+            j = r // 2 - i
 
             @pl.when((j >= 0) & (j < slabs))
             def _():
                 @pl.when(t >= 1)
                 def _():
                     for direction in range(2):
-                        gu_copy(r - 1, direction, t - 1).wait_recv()
+                        gu_copy(j, direction, t - 1).wait_recv()
                         mine_ref = gu_ref(j, direction, t)
-                        got = gu_slot[direction, lax.rem(r + 1, 2), t - 1].astype(F32)
+                        got = gu_slot[direction, lax.rem(j, 2), t - 1].astype(F32)
                         mine_ref[...] = (got + mine_ref[...].astype(F32)).astype(BF16)
-
-            @pl.when((t <= n - 2) & (j >= 1) & (j <= slabs))
-            def _():
-                for direction in range(2):
-                    gu_copy(r - 1, direction, t).wait_send()
-
-            @pl.when((j >= 0) & (j < slabs) & (t <= n - 2))
-            def _():
-                for direction in range(2):
-                    gu_copy(r, direction, t).start()
+                    for direction in range(2):
+                        gu_copy(j, direction, t - 1).wait_send()
+
+                @pl.when(t <= n - 2)
+                def _():
+                    for direction in range(2):
+                        gu_copy(j, direction, t).start()
             return 0
 
-        lax.fori_loop(0, n, tick, 0)
+        lax.fori_loop(0, n // 2, tick, 0)
 
     parts = d // 128
 
@@ -262,46 +260,56 @@
 
         lax.fori_loop(0, parts, part, 0)
 
-    def backward(layer, c):
+    def backward(layer, c, between_halves):
         def tile(k, _):
             r = pl.ds(pl.multiple_of(k * TILE, TILE), TILE)
-            gate = dot(a[layer, r, :], wgu[layer, 0, :, cols(c)])
-            up = dot(a[layer, r, :], wgu[layer, 1, :, cols(c)])
+            wide = jnp.concatenate([wgu[layer, 0, :, cols(c)], wgu[layer, 1, :, cols(c)]], 1)
+            both = dot(a[layer, r, :], wide)
+            gate, up = both[:, :CHUNK], both[:, CHUNK:]
             by = dot_t(dy[r, :], wd[layer, cols(c), :]).astype(BF16).astype(F32)
             sig = jax.nn.sigmoid(gate)
             silu = gate * sig
             hid[r, :] = (silu * up).astype(BF16)
             by_gate = (by * up * (sig + silu * (1.0 - sig))).astype(BF16)
             by_up = (by * silu).astype(BF16)
-            dgdu[r, pl.ds(0, CHUNK)] = by_gate
-            dgdu[r, pl.ds(CHUNK, CHUNK)] = by_up
+            by_both = jnp.concatenate([by_gate, by_up], 1)
+            dgdu[r, :] = by_both
             if layer == 1:
-                out = dot_t(by_gate, wgu[layer, 0, :, cols(c)]) + dot_t(by_up, wgu[layer, 1, :, cols(c)])
-
-                @pl.when(c == 0)
-                def _():
-                    acc[r, :] = out
-
-                @pl.when(c > 0)
-                def _():
-                    acc[r, :] += out
+                acc[r, :] += dot_t(by_both, wide)
             return 0
 
         lax.fori_loop(0, tokens // TILE, tile, 0)
+        between_halves()
         by_w = dot(at[...], dgdu[...])
         dgu[layer, 0, :, cols(c)] = by_w[:, :CHUNK].astype(BF16)
         dgu[layer, 1, :, cols(c)] = by_w[:, CHUNK:].astype(BF16)
         dd[layer, cols(c), :] = dot(dyt[...], hid[...]).T.astype(BF16)
 
     def last_layer(c, _):
-        backward(1, c)
-        gu_round(c)
+        def between_halves():
+            @pl.when(c >= 1)
+            def _():
+                gu_round(2 * c - 1)
+
+        backward(1, c, between_halves)
+        gu_round(2 * c)
         return 0
 
     lax.fori_loop(0, chunks, last_layer, 0)
+
+    early = min(2, steps)
 
     def norm_back(k, _):
         r = small(k)
+
+        @pl.when(k == 0)
+        def _():
+            dn_round(1, 0)
+
+        @pl.when(k == steps // 2)
+        def _():
+            gu_round(2 * chunks - 1)
+            dn_round(1, 1)
         by_a = acc[r, :].astype(BF16).astype(F32)
         wide = h[r, :].astype(F32)
         scale = scale_of(wide)
@@ -316,17 +324,27 @@
     lax.fori_loop(0, steps, norm_back, 0)
 
     def first_layer(c, _):
-        backward(0, c)
-        gu_round(chunks + c)
-        dn_round(1, c)
+        def between_halves():
+            @pl.when(c >= 1)
+            def _():
+                gu_round(2 * (chunks + c) - 1)
+
+        backward(0, c, between_halves)
+        gu_round(2 * (chunks + c))
+
+        @pl.when(c + early < n)
+        def _():
+            dn_round(1, c + early)
         return 0
 
     lax.fori_loop(0, chunks, first_layer, 0)
-    for t in range(chunks, n):
+    for t in range(chunks + early, n):
         dn_round(1, t)
 
     def drain(k, _):
-        gu_round(2 * chunks + k)
+        @pl.when(k < n - 1)
+        def _():
+            gu_round(2 * slabs - 1 + k)
         dn_round(0, k)
         return 0
 
@@ -410,7 +428,7 @@
             dma((2, 3, 2, 2)),
             dma((2, 3, 2, 2)),
             dma((2, 2, n - 1)),
-            dma((2, n - 1)),
+            dma((2, 2, n - 1)),
             dma((2, 2, 2, d // 128)),
             dma((2, 2, d // 128)),
             dma((n - 1,)),

time: 304 us -> 291 us (0.957)
  Pallas kernels: 293 us -> 280 us
    pallas_call x1, Pallas kernels: 293 us -> 280 us  [summed_gradients(): pl.pallas_call(functools.partial(kernel, n, dims), out_shape=(jax.ShapeDt...]
where the time goes in v2:
time: 291 us; the launch traced here: 290 us
  Pallas kernels  280 us (96%)
  other arithmetic  8.11 us (3%)
    pallas_call x1, Pallas kernels, summed_gradients(): pl.pallas_call(functools.partial(kernel, n, dims), out_shape=(jax.ShapeDt...  280 us
    convert_element_type x2, other arithmetic, adamw(): return ((w - 0.02 * step).astype(BF16), m, v)  8.11 us

profile of v2, /device:TPU:22, one launch (start us, length us, event | category | flops | bytes accessed | tf_op | source)
XLA Modules:
  0.0 290.4 jit_solution(12154455506511187509)
XLA Ops:
  0.6 279.7 %shard_map.178 = (bf16[2,80,1792]{2,1,0:T(8,128)(2,1)}, bf16[2,80,1792]{2,1,0:T(8,128)(2,1)}, bf16[2,224,640]{2,1,0:T(8,128)(2,1)}, f32[8,128]{1,0:T(8,128)}) custom-call(bf16[1,2048,640]{2,1,0:T(8,128)(2,1)} %x_hbm.1, bf16[1,2048,640]{2,1,0:T(8,128)(2,1)} %dy_hbm.1, bf16[2,80,1792]{2,1,0:T(8,128)(2,1)} %wg_hbm.1, bf16[2,80,1792]{2,1,0:T(8,128)(2,1)} %wu_hbm.1, ...), custom_call_target="tpu_custom_call" | custom-call | tf_op jit(solution)/shard_map/pallas_call | solution.py:397
  280.4 1.2 slice.3
  282.3 0.0 copy-start
  282.3 0.0 copy-start.1
  282.3 0.0 copy-start.2
  282.3 0.0 copy-start.3
  282.3 6.2 %fusion.2 = (bf16[2,80,1792]{2,1,0:T(8,128)(2,1)}, f32[2,80,1792]{2,1,0:T(8,128)}, f32[2,80,1792]{2,1,0:T(8,128)}, bf16[2,80,1792]{2,1,0:T(8,128)(2,1)}, f32[2,80,1792]{2,1,0:T(8,128)}, /*index=5*/f32[2,80,1792]{2,1,0:T(8,128)}) fusion(bf16[2,80,1792]{2,1,0:T(8,128)(2,1)} %wg_hbm.1, f32[]{:T(128)} %bitcast, bf16[2,80,1792]{2,1,0:T(8,128)(2,1)} %get-tuple-element.13, ...), kind=kLoop, calls=%fused_computation.11 | loop fusion | flops 9748480 | bytes 12615684 | tf_op jit(solution)/shard_map/convert_element_type | solution.py:445
  288.5 0.0 copy-done
  288.5 0.0 copy-done.1
  288.5 0.0 copy-done.2
  288.5 0.0 copy-done.3
  288.5 1.9 fusion.8
Async XLA Ops:
  282.3 6.3 %copy-start = (bf16[2,224,640]{2,1,0:T(8,128)(2,1)S(1)}, bf16[2,224,640]{2,1,0:T(8,128)(2,1)}, u32[]{:S(2)}) copy-start(bf16[2,224,640]{2,1,0:T(8,128)(2,1)} %wd_hbm.1) | copy-start | bytes 1720324
  282.3 6.2 %copy-start.1 = (f32[2,224,640]{2,1,0:T(8,128)S(1)}, f32[2,224,640]{2,1,0:T(8,128)}, u32[]{:S(2)}) copy-start(f32[2,224,640]{2,1,0:T(8,128)} %param.21) | copy-start | bytes 3440644
  282.3 6.2 %copy-start.2 = (f32[2,224,640]{2,1,0:T(8,128)S(1)}, f32[2,224,640]{2,1,0:T(8,128)}, u32[]{:S(2)}) copy-start(f32[2,224,640]{2,1,0:T(8,128)} %param.18) | copy-start | bytes 3440644
  282.3 6.2 %copy-start.3 = (bf16[2,224,640]{2,1,0:T(8,128)(2,1)S(1)}, bf16[2,224,640]{2,1,0:T(8,128)(2,1)}, u32[]{:S(2)}) copy-start(bf16[2,224,640]{2,1,0:T(8,128)(2,1)} %get-tuple-element.16) | copy-start | bytes 1720324

commit v3 on v2

--- a/solution.py
+++ b/solution.py
@@ -28,7 +28,7 @@
 
 def kernel(n, dims, x_hbm, dy_hbm, wg_hbm, wu_hbm, wd_hbm, gg_hbm, gu_hbm, gd_hbm, total_ref,
            wgu, wd, dgu, dd, h, dy, a, at, dyt, acc, hid, dgdu, gu_slot, dn_slot, squares, mine,
-           load_sem, out_sem, zrecv, zsend, drecv, dsend, gu_recv, gu_send, dn_recv, dn_send, sq_recv, sq_send):
+           load_sem, out_sem, zrecv, zsend, drecv, dsend, yrecv, ysend, erecv, esend, gu_recv, gu_send, dn_recv, dn_send, sq_recv, sq_send):
     tokens, d, ff, rows, down = dims
     half = down // 2
     chunks = ff // CHUNK
@@ -36,6 +36,8 @@
     rep = lax.axis_index("rep")
     core = lax.rem(rep, 2)
     partner = rep + 1 - 2 * core
+    side = lax.rem(rep // 2, 2)
+    beside = rep + 2 - 4 * side
     ahead = (lax.rem(me + 1, n), lax.rem(me + n - 1, n))
 
     def to(direction):
@@ -56,77 +58,85 @@
     for k in range(1, n):
         pl.semaphore_signal(barrier, inc=1, device_id={"dp": lax.rem(me + k, n)}, device_id_type=MESH)
     pl.semaphore_signal(barrier, inc=1, device_id={"rep": partner}, device_id_type=MESH)
-    pl.semaphore_wait(barrier, n)
+    pl.semaphore_signal(barrier, inc=1, device_id={"rep": beside}, device_id_type=MESH)
+    pl.semaphore_wait(barrier, n + 1)
     for one in loads[:6]:
         one.wait()
 
-    def piece(layer, which, number, direction, block):
+    lanes = ff // 128
+    ahead_cut = (lanes // 2 + 1) // 2 * 128
+    gu_size = (ahead_cut, ff // 2 - ahead_cut)
+    dn_size = (half // 16 // 2 * 16, half - half // 16 // 2 * 16)
+    dn_cut = (d // 128 + 1) // 2 * 128
+    pieces = 4
+
+    def piece(layer, matrix, which, number, direction, block):
         if number < 2:
-            wide = ff // 2
-            cut = (wide // 128 + 1) // 2 * 128
-            off, size = (0, cut) if number == 0 else (cut, wide - cut)
-            return wgu.at[layer, which, pl.ds(pl.multiple_of(block * rows, 16), rows), pl.ds(direction * wide + off, size)]
-        cut = (half // 16 + 1 - layer) // 2 * 16
-        off, size = (0, cut) if direction == 0 else (cut, half - cut)
-        return wd.at[layer, pl.ds(pl.multiple_of(block * down + which * half + off, 16), size), :]
+            size = gu_size[direction]
+            cut = (size // 128 + 1) // 2 * 128
+            off, size_ = (0, cut) if number == 0 else (cut, size - cut)
+            start = (2 * gu_size[0] if direction else 0) + which * size + off
+            r = pl.ds(pl.multiple_of(block * rows, 16), rows)
+            return wgu.at[layer, matrix, r, pl.ds(pl.multiple_of(start, 128), size_)]
+        start = block * down + which * half + (dn_size[0] if direction else 0)
+        lane = pl.ds(0, dn_cut) if number == 2 else pl.ds(dn_cut, d - dn_cut)
+        return wd.at[layer, pl.ds(pl.multiple_of(start, 16), dn_size[direction]), lane]
 
     def held(direction, t):
         return lax.rem(me - t + n, n) if direction == 0 else lax.rem(me + t, n)
 
+    def send(ref, out_sem, in_sem, layer, number, direction, t, device):
+        slot = lax.rem(t, 2)
+        return pltpu.make_async_remote_copy(ref, ref, out_sem.at[layer, number, direction, slot], in_sem.at[layer, number, direction, slot],
+                                            device_id=device, device_id_type=MESH)
+
     def along(layer, number, direction, t):
-        ref = piece(layer, core, number, direction, held(direction, t))
-        slot = lax.rem(t, 2)
-        return pltpu.make_async_remote_copy(ref, ref, zsend.at[layer, number, direction, slot], zrecv.at[layer, number, direction, slot],
-                                            device_id=to(direction), device_id_type=MESH)
+        ref = piece(layer, side, core, number, direction, held(direction, t))
+        return send(ref, zsend, zrecv, layer, number, direction, t, to(direction))
+
+    def arrived(layer, number, direction, t):
+        ref = piece(layer, side, core, number, direction, held(direction, t))
+        return send(ref, zsend, zrecv, layer, number, direction, t - 1, to(direction))
 
     def across(layer, which, number, direction, t):
-        ref = piece(layer, which, number, direction, held(direction, t))
-        slot = lax.rem(t, 2)
-        return pltpu.make_async_remote_copy(ref, ref, dsend.at[layer, number, direction, slot], drecv.at[layer, number, direction, slot],
-                                            device_id={"rep": partner}, device_id_type=MESH)
-
-    def arrived(layer, number, direction, t):
-        ref = piece(layer, core, number, direction, held(direction, t))
-        slot = lax.rem(t + 1, 2)
-        return pltpu.make_async_remote_copy(ref, ref, zsend.at[layer, number, direction, slot], zrecv.at[layer, number, direction, slot],
-                                            device_id=to(direction), device_id_type=MESH)
+        ref = piece(layer, side, which, number, direction, held(direction, t))
+        return send(ref, dsend, drecv, layer, number, direction, t, {"rep": partner})
+
+    def over(layer, matrix, number, direction, t):
+        ref = piece(layer, matrix, core, number, direction, held(direction, t))
+        return send(ref, ysend, yrecv, layer, number, direction, t, {"rep": beside})
+
+    def onward(layer, which, number, direction, t):
+        ref = piece(layer, 1 - side, which, number, direction, held(direction, t))
+        return send(ref, esend, erecv, layer, number, direction, t, {"rep": partner})
+
+    def when(condition, f):
+        pl.when(condition)(f)
 
     def gather_round(layer, t):
-        for number in range(3):
+        for number in range(pieces):
             for direction in range(2):
-                @pl.when(t >= 1)
-                def _():
-                    arrived(layer, number, direction, t).wait_recv()
-
-                @pl.when((t >= 2) & (t < n))
-                def _():
-                    across(layer, 1 - core, number, direction, t - 1).wait_recv()
-
+                when((t >= 1) & (t < n), lambda: arrived(layer, number, direction, t).wait_recv())
+                when((t >= 2) & (t <= n), lambda: across(layer, 1 - core, number, direction, t - 1).wait_recv())
             for direction in range(2):
-                @pl.when((t >= 2) & (t <= n - 2))
-                def _():
-                    along(layer, number, direction, t - 2).wait_send()
-
-                @pl.when(t <= n - 2)
-                def _():
-                    along(layer, number, direction, t).start()
-
-                @pl.when(t >= 3)
-                def _():
-                    across(layer, core, number, direction, t - 2).wait_send()
-
-                @pl.when(t >= 1)
-                def _():
-                    across(layer, core, number, direction, t).start()
+                when((t >= 2) & (t <= n), lambda: along(layer, number, direction, t - 2).wait_send())
+                when(t <= n - 2, lambda: along(layer, number, direction, t).start())
+                when(t >= 3, lambda: across(layer, core, number, direction, t - 2).wait_send())
+                when((t >= 1) & (t < n), lambda: across(layer, core, number, direction, t).start())
+        for number in range(2):
+            for direction in range(2):
+                when((t >= 2) & (t <= n), lambda: over(layer, 1 - side, number, direction, t - 1).wait_recv())
+                when(t >= 3, lambda: onward(layer, 1 - core, number, direction, t - 2).wait_recv())
+            for direction in range(2):
+                when(t >= 3, lambda: over(layer, side, number, direction, t - 2).wait_send())
+                when((t >= 1) & (t < n), lambda: over(layer, side, number, direction, t).start())
+                when(t >= 4, lambda: onward(layer, core, number, direction, t - 3).wait_send())
+                when((t >= 2) & (t <= n), lambda: onward(layer, core, number, direction, t - 1).start())
 
     def gather_end(layer):
-        for number in range(3):
+        for number in range(2):
             for direction in range(2):
-                across(layer, 1 - core, number, direction, n - 1).wait_recv()
-                for t in (n - 3, n - 2):
-                    along(layer, number, direction, t).wait_send()
-                for t in (n - 2, n - 1):
-                    across(layer, core, number, direction, t).wait_send()
+                onward(layer, core, number, direction, n - 1).wait_send()
 
     def small(k):
         return pl.ds(pl.multiple_of(k * SMALL, SMALL), SMALL)
@@ -150,7 +160,7 @@
             acc[small(t), :] = jnp.zeros((SMALL, d), F32)
         return 0
 
-    lax.fori_loop(0, max(n, steps), first, 0)
+    lax.fori_loop(0, max(n + 2, steps), first, 0)
     gather_end(0)
 
     def cols(c):
@@ -186,6 +196,8 @@
         return 0
 
     lax.fori_loop(0, steps, between, 0)
+    for t in (n, n + 1):
+        gather_round(1, t)
     gather_end(1)
 
     slabs = 2 * chunks
@@ -262,6 +274,7 @@
 
     def backward(layer, c, between_halves):
         def tile(k, _):
+            pl.when(k == tokens // TILE - 1)(between_halves)
             r = pl.ds(pl.multiple_of(k * TILE, TILE), TILE)
             wide = jnp.concatenate([wgu[layer, 0, :, cols(c)], wgu[layer, 1, :, cols(c)]], 1)
             both = dot(a[layer, r, :], wide)
@@ -279,7 +292,6 @@
             return 0
 
         lax.fori_loop(0, tokens // TILE, tile, 0)
-        between_halves()
         by_w = dot(at[...], dgdu[...])
         dgu[layer, 0, :, cols(c)] = by_w[:, :CHUNK].astype(BF16)
         dgu[layer, 1, :, cols(c)] = by_w[:, CHUNK:].astype(BF16)
@@ -423,10 +435,14 @@
             pltpu.VMEM((8, 128), F32),
             dma((8,)),
             dma((6,)),
-            dma((2, 3, 2, 2)),
-            dma((2, 3, 2, 2)),
-            dma((2, 3, 2, 2)),
-            dma((2, 3, 2, 2)),
+            dma((2, 4, 2, 2)),
+            dma((2, 4, 2, 2)),
+            dma((2, 4, 2, 2)),
+            dma((2, 4, 2, 2)),
+            dma((2, 2, 2, 2)),
+            dma((2, 2, 2, 2)),
+            dma((2, 2, 2, 2)),
+            dma((2, 2, 2, 2)),
             dma((2, 2, n - 1)),
             dma((2, 2, n - 1)),
             dma((2, 2, 2, d // 128)),

time: 291 us -> 279 us (0.959)
  Pallas kernels: 280 us -> 268 us
    pallas_call x1, Pallas kernels: 280 us -> 268 us  [summed_gradients(): pl.pallas_call(functools.partial(kernel, n, dims), out_shape=(jax.ShapeDt...]
where the time goes in v3:
time: 279 us
  Pallas kernels  268 us (96%)
  other arithmetic  8.11 us (3%)
    pallas_call x1, Pallas kernels, summed_gradients(): pl.pallas_call(functools.partial(kernel, n, dims), out_shape=(jax.ShapeDt...  268 us
    convert_element_type x2, other arithmetic, adamw(): return ((w - 0.02 * step).astype(BF16), m, v)  8.11 us

profile of v3, /device:TPU:22, one launch (start us, length us, event | category | flops | bytes accessed | tf_op | source)
XLA Modules:
  0.0 279.1 jit_solution(10045674677498722296)
XLA Ops:
  0.6 268.3 %shard_map.178 = (bf16[2,80,1792]{2,1,0:T(8,128)(2,1)}, bf16[2,80,1792]{2,1,0:T(8,128)(2,1)}, bf16[2,224,640]{2,1,0:T(8,128)(2,1)}, f32[8,128]{1,0:T(8,128)}) custom-call(bf16[1,2048,640]{2,1,0:T(8,128)(2,1)} %x_hbm.1, bf16[1,2048,640]{2,1,0:T(8,128)(2,1)} %dy_hbm.1, bf16[2,80,1792]{2,1,0:T(8,128)(2,1)} %wg_hbm.1, bf16[2,80,1792]{2,1,0:T(8,128)(2,1)} %wu_hbm.1, ...), custom_call_target="tpu_custom_call" | custom-call | tf_op jit(solution)/shard_map/pallas_call | solution.py:409
  269.0 1.2 slice.3
  270.9 0.0 copy-start
  270.9 0.0 copy-start.1
  270.9 0.0 copy-start.2
  270.9 0.0 copy-start.3
  270.9 6.2 %fusion.2 = (bf16[2,80,1792]{2,1,0:T(8,128)(2,1)}, f32[2,80,1792]{2,1,0:T(8,128)}, f32[2,80,1792]{2,1,0:T(8,128)}, bf16[2,80,1792]{2,1,0:T(8,128)(2,1)}, f32[2,80,1792]{2,1,0:T(8,128)}, /*index=5*/f32[2,80,1792]{2,1,0:T(8,128)}) fusion(bf16[2,80,1792]{2,1,0:T(8,128)(2,1)} %wg_hbm.1, f32[]{:T(128)} %bitcast, bf16[2,80,1792]{2,1,0:T(8,128)(2,1)} %get-tuple-element.13, ...), kind=kLoop, calls=%fused_computation.11 | loop fusion | flops 9748480 | bytes 12615684 | tf_op jit(solution)/shard_map/convert_element_type | solution.py:461
  277.1 0.0 copy-done
  277.1 0.0 copy-done.1
  277.1 0.0 copy-done.2
  277.1 0.0 copy-done.3
  277.2 1.9 fusion.8
Async XLA Ops:
  270.9 6.3 %copy-start = (bf16[2,224,640]{2,1,0:T(8,128)(2,1)S(1)}, bf16[2,224,640]{2,1,0:T(8,128)(2,1)}, u32[]{:S(2)}) copy-start(bf16[2,224,640]{2,1,0:T(8,128)(2,1)} %wd_hbm.1) | copy-start | bytes 1720324
  270.9 6.2 %copy-start.1 = (f32[2,224,640]{2,1,0:T(8,128)S(1)}, f32[2,224,640]{2,1,0:T(8,128)}, u32[]{:S(2)}) copy-start(f32[2,224,640]{2,1,0:T(8,128)} %param.21) | copy-start | bytes 3440644
  270.9 6.2 %copy-start.2 = (f32[2,224,640]{2,1,0:T(8,128)S(1)}, f32[2,224,640]{2,1,0:T(8,128)}, u32[]{:S(2)}) copy-start(f32[2,224,640]{2,1,0:T(8,128)} %param.18) | copy-start | bytes 3440644
  270.9 6.2 %copy-start.3 = (bf16[2,224,640]{2,1,0:T(8,128)(2,1)S(1)}, bf16[2,224,640]{2,1,0:T(8,128)(2,1)}, u32[]{:S(2)}) copy-start(bf16[2,224,640]{2,1,0:T(8,128)(2,1)} %get-tuple-element.16) | copy-start | bytes 1720324
